TPU v7x, 32 devices: a whole 2x2x4 slice. The times are simulated.
32 devices in a mesh: tm: 4 (over y, core), space: 8 (over z, x).
Axes of the slice: x: 2, y: 2, z: 4, core: 2. Of those that a mesh axis runs over, the one named last changes fastest.
Arguments:
- perm_field: float32 [4, 32, 32, 256], P(None, 'space'), may hold values from 0.5 to 2
- step_multiplier: float32 [4, 32, 32, 256], P('tm', 'space'), may hold values from 0.5 to 2
- inflow: float32 [4, 32, 32, 256], P('tm', 'space'), may hold values from -3 to 3
- start_pressure: float32 [32, 32, 256], P('space'), may hold values from -6 to 6
- start_saturation: float32 [32, 32, 256], P('space'), may hold values from 0.1 to 0.9
- region_ids: int32 [32, 32, 256], P('space'), may hold values from 0 to 7
- region_table: float32 [3, 8], replicated, may hold values from 0.25 to 2
- well_cells: int32 [32], replicated, may hold values from 0 to 262143
- well_rates: float32 [4, 32], P('tm'), may hold values from -8 to 8
- observed: float32 [4, 4, 32], P(None, 'tm'), may hold values from -6 to 6
Outputs:
- misfit: float32 [4], replicated
- slab_pressure: float32 [4, 4, 32, 32, 256], P('tm', None, 'space')
- slab_saturation: float32 [4, 4, 32, 32, 256], P('tm', None, 'space')
All inputs are finite; a program needn't handle non-finite values.
Results may differ from a plain program's by a relative error of at most 0.0003.
Values sent between devices are 32-bit elements; how exact they have to be, the bound alone decides.
A program may use at most 64 MiB of HBM per device.

v0:
```python
import jax
import jax.numpy as jnp
from jax import lax
from jax.sharding import PartitionSpec as P

MB = 1
REP_DEV = 1
ITERS = 3


def padded(cells, sides, width):
    for axis, dim in sides:
        count = lax.axis_size(axis)
        ends = count - 1
        head = lax.slice_in_dim(cells, 0, width, axis=dim)
        tail = lax.slice_in_dim(cells, cells.shape[dim] - width, cells.shape[dim], axis=dim)
        cells = jnp.concatenate(
            [
                lax.ppermute(tail, axis, [(i, (i + 1) % count) for i in range(ends)]),
                cells,
                lax.ppermute(head, axis, [((i + 1) % count, i) for i in range(ends)]),
            ],
            axis=dim,
        )
    return cells


def shifted(values, dimension, offset):
    margins = [(0, 0)] * values.ndim
    length = values.shape[dimension]
    if offset > 0:
        margins[dimension] = (1, 0)
        return lax.slice_in_dim(jnp.pad(values, margins), 0, length, axis=dimension)
    margins[dimension] = (0, 1)
    return lax.slice_in_dim(jnp.pad(values, margins), 1, length + 1, axis=dimension)


def neighbour_values(values_ext):
    middle = values_ext[:, 1:-1]
    return (
        values_ext[:, :-2],
        values_ext[:, 2:],
        shifted(middle, 2, 1),
        shifted(middle, 2, -1),
        shifted(middle, 3, 1),
        shifted(middle, 3, -1),
    )


def coefficients(conduct_ext):
    middle = conduct_ext[:, 1:-1]
    others = neighbour_values(conduct_ext)
    links = [jnp.sqrt(middle * other_side) for other_side in others]
    link_total = links[0] + links[1] + links[2] + links[3] + links[4] + links[5]
    return tuple(links) + (link_total,)


def jacobi_sweep(pressure_ext, couplings, storage, right_side):
    beside = neighbour_values(pressure_ext)
    inflowing = couplings[0] * beside[0]
    for link_index in range(1, 6):
        inflowing = inflowing + couplings[link_index] * beside[link_index]
    divisor = jnp.where(storage > 0, storage + couplings[6], 1.0)
    return (right_side + inflowing) / divisor


def fraction(saturation, ratio):
    squared = saturation * saturation
    remain = (1.0 - saturation) * (1.0 - saturation)
    return squared / (squared + ratio * remain)


def transport(pressure_ext, flow_ext, couplings, saturation, gain, source):
    centre_p = pressure_ext[:, 1:-1]
    centre_f = flow_ext[:, 1:-1]
    other_p = neighbour_values(pressure_ext)
    other_f = neighbour_values(flow_ext)
    outflow = None
    for link_index in range(6):
        face_flux = couplings[link_index] * (centre_p - other_p[link_index])
        carried = face_flux * jnp.where(face_flux > 0, centre_f, other_f[link_index])
        outflow = carried if outflow is None else outflow + carried
    gained = (
        jnp.maximum(source, 0.0) * (1.0 - saturation)
        - jnp.maximum(-source, 0.0) * centre_f
        - outflow
    )
    return saturation + gain * gained


def region_fields(region_ids, region_table):
    fields = []
    for table_row in range(3):
        summed = jnp.zeros(region_ids.shape, jnp.float32)
        for region_index in range(region_table.shape[1]):
            summed = summed + jnp.where(
                region_ids == region_index, region_table[table_row, region_index], 0.0
            )
        fields.append(summed)
    return (fields[0], fields[1], 0.1 * fields[2])


def advance(pressure, saturation, conduct, source, inflow_now, storage, ratio, gain):
    right_side = storage * pressure + source + inflow_now
    flow_frac = fraction(saturation, ratio)
    edges = padded(jnp.stack([conduct, pressure]), (("space", 2),), 1)
    couplings = coefficients(edges[0])
    iterate_ext = edges[1]
    iterate = pressure
    for sweep_index in range(ITERS):
        if sweep_index > 0:
            iterate_ext = padded(iterate, (("space", 1),), 1)
        iterate = jacobi_sweep(iterate_ext, couplings, storage, right_side)
    both = padded(jnp.stack([iterate, flow_frac]), (("space", 2),), 1)
    saturation = transport(both[0], both[1], couplings, saturation, gain, source)
    return (iterate, saturation)


def body(
    perm_field,
    step_multiplier,
    inflow,
    start_pressure,
    start_saturation,
    region_ids,
    region_table,
    well_cells,
    well_rates,
    observed,
):
    sections = lax.axis_size("tm")
    section_index = lax.axis_index("tm")
    space_index = lax.axis_index("space")
    grid_shape = start_pressure.shape
    width_x, depth, across = grid_shape
    batch_size = MB
    storage, ratio, gain = region_fields(region_ids, region_table)
    layer_ids = lax.broadcasted_iota(jnp.int32, grid_shape, 0) + space_index * width_x
    cell_ids = (
        layer_ids * depth + lax.broadcasted_iota(jnp.int32, grid_shape, 1)
    ) * across + lax.broadcasted_iota(jnp.int32, grid_shape, 2)
    well_picks = (well_cells[:, None] == cell_ids.reshape(1, -1)).astype(jnp.float32)
    well_owned = jnp.sum(well_picks, axis=1)
    start_p = jnp.broadcast_to(start_pressure, (batch_size,) + grid_shape)
    start_s = jnp.broadcast_to(start_saturation, (batch_size,) + grid_shape)

    def mismatch(pressure, measured):
        predicted = jnp.dot(
            pressure.reshape(batch_size, -1), well_picks.T, precision=lax.Precision.HIGHEST
        )
        return jnp.sum(well_owned * (predicted - measured) ** 2, axis=1)

    misfit = jnp.zeros((perm_field.shape[0],), jnp.float32)
    fields = (
        lax.all_gather(step_multiplier, "tm", axis=0, tiled=True),
        lax.all_gather(inflow, "tm", axis=0, tiled=True),
        lax.all_gather(well_rates, "tm", axis=0, tiled=True),
    )
    measured_all = lax.all_to_all(observed, "tm", split_axis=0, concat_axis=1, tiled=True)
    perm_rows = lax.dynamic_slice_in_dim(perm_field, section_index * batch_size, batch_size, 0)
    rate_rows = fields[2]
    placed = jnp.dot(rate_rows, well_picks, precision=lax.Precision.HIGHEST)
    all_sources = placed.reshape((rate_rows.shape[0],) + grid_shape)
    zero_ends = jnp.zeros((sections, batch_size) + grid_shape, jnp.float32)

    def one_section(slab_index, state_tuple):
        pressure, saturation, ends_p, ends_s, errors = state_tuple
        position = slab_index * REP_DEV + 0
        multiplier = lax.dynamic_index_in_dim(fields[0], position, 0, keepdims=False)
        inflow_now = lax.dynamic_index_in_dim(fields[1], position, 0, keepdims=False)
        source = lax.dynamic_index_in_dim(all_sources, position, 0, keepdims=False)
        pressure, saturation = advance(
            pressure, saturation, perm_rows * multiplier, source, inflow_now, storage, ratio, gain
        )
        errors = errors + mismatch(
            pressure, lax.dynamic_index_in_dim(measured_all, position, 1, keepdims=False)
        )
        ends_p = lax.dynamic_update_index_in_dim(ends_p, pressure, slab_index, 0)
        ends_s = lax.dynamic_update_index_in_dim(ends_s, saturation, slab_index, 0)
        return (pressure, saturation, ends_p, ends_s, errors)

    result = lax.fori_loop(
        0,
        sections,
        one_section,
        (start_p, start_s, zero_ends, zero_ends, jnp.zeros((batch_size,), jnp.float32)),
    )
    slab_pressure, slab_saturation = (
        lax.all_to_all(result[2], "tm", split_axis=0, concat_axis=1, tiled=True),
        lax.all_to_all(result[3], "tm", split_axis=0, concat_axis=1, tiled=True),
    )
    misfit = lax.dynamic_update_slice_in_dim(misfit, result[4], section_index * batch_size, 0)
    totals = lax.psum(misfit, ("tm", "space"))
    return (totals / (sections * REP_DEV * well_cells.shape[0]), slab_pressure, slab_saturation)


def solution(mesh):
    return jax.shard_map(
        body,
        mesh=mesh,
        in_specs=(
            P(None, "space", None, None),
            P("tm", "space", None, None),
            P("tm", "space", None, None),
            P("space", None, None),
            P("space", None, None),
            P("space", None, None),
            P(),
            P(),
            P("tm", None),
            P(None, "tm", None),
        ),
        out_specs=(P(), P("tm", None, "space", None, None), P("tm", None, "space", None, None)),
        check_vma=False,
    )
```

profile of v0, /device:TPU:0, one launch (start us, length us, event | category | flops | bytes accessed | tf_op | source)
XLA Modules:
  0.0 281.1 jit_solution(10147886916045654952)
XLA Ops:
  6.7 5.2 %all-gather = f32[4,1,32]{2,1,0:T(1,128)S(1)} all-gather(f32[1,1,32]{2,1,0:T(1,128)S(1)} %bitcast.154), channel_id=1, replica_groups=mesh['tm'=4,'space'=8] {'tm'}, dimensions={0}, use_global_device_ids=true | all-gather | bytes 640 | tf_op jit(solution)/shard_map/all_gather | solution.py:157
  13.9 8.2 %all_gather.10 = f32[4,4,32,256]{3,2,1,0:T(8,128)} all-gather(f32[1,4,32,256]{3,2,1,0:T(8,128)S(1)} %copy-done.7), channel_id=1, replica_groups=mesh['tm'=4,'space'=8] {'tm'}, dimensions={0}, use_global_device_ids=true | all-gather | bytes 655360 | tf_op jit(solution)/shard_map/all_gather | solution.py:156
  22.1 7.4 %all_gather.11 = f32[4,4,32,256]{3,2,1,0:T(8,128)S(1)} all-gather(f32[1,4,32,256]{3,2,1,0:T(8,128)S(1)} %copy-done.8), channel_id=1, replica_groups=mesh['tm'=4,'space'=8] {'tm'}, dimensions={0}, use_global_device_ids=true | all-gather | bytes 655360 | tf_op jit(solution)/shard_map/all_gather | solution.py:155
  29.6 5.2 %select_add_fusion = (f32[4,32,256]{2,1,0:T(8,128)S(1)}, pred[4,32,256]{2,1,0:T(8,128)(4,1)S(1)}, pred[4,32,256]{2,1,0:T(8,128)(4,1)S(1)}, pred[4,32,256]{2,1,0:...) fusion(f32[]{:T(128)} %bitcast.28, f32[]{:T(128)} %bitcast.27, ...), kind=kLoop, calls=%fused_computation.152 | loop fusion | flops 753664 | bytes 524320 | tf_op jit(solution)/shard_map/add | solution.py:96
  34.8 5.1 %add_multiply_fusion = f32[4,32,256]{2,1,0:T(8,128)S(1)} fusion(pred[4,32,256]{2,1,0:T(8,128)(4,1)S(1)} %get-tuple-element.474, pred[4,32,256]{2,1,0:T(8,128)(4,1)S(1)} %get-tuple-element.473, pred[4,32,256]{2,1,0:T(8,128)(4,1)S(1)} %get-tuple-element.472, pred[4,32,256]{2,1,0:T(8,128)(4,1)S(1)} %get-tuple-element.471, ...), kind=kLoop, calls=%fused_computation.153 | loop fusion | flops 524288 | bytes 393248 | tf_op jit(solution)/shard_map/mul | solution.py:100
  39.8 5.1 %select_add_fusion.1 = f32[4,32,256]{2,1,0:T(8,128)S(1)} fusion(pred[4,32,256]{2,1,0:T(8,128)(4,1)S(1)} %get-tuple-element.474, pred[4,32,256]{2,1,0:T(8,128)(4,1)S(1)} %get-tuple-element.473, pred[4,32,256]{2,1,0:T(8,128)(4,1)S(1)} %get-tuple-element.472, pred[4,32,256]{2,1,0:T(8,128)(4,1)S(1)} %get-tuple-element.471, ...), kind=kLoop, calls=%fused_computation.155 | loop fusion | flops 491520 | bytes 393248 | tf_op jit(solution)/shard_map/add | solution.py:96
  46.0 170.8 %while.24 = (s32[]{:T(128)}, f32[1,4,32,256]{3,2,1,0:T(8,128)S(1)}, f32[1,4,32,256]{3,2,1,0:T(8,128)S(1)}, f32[4,1,4,32,256]{4,3,2,1,0:T(8,128)}, f32[4,1,4,32,2...) while((s32[]{:T(128)}, f32[1,4,32,256]{3,2,1,0:T(8,128)S(1)}, ...), condition=%wide.region_3.4_spmd.clone, body=%wide.region_1.3_spmd.clone.sunk | while | flops 19529856 | bytes 16516069 | solution.py:182
  56.7 5.1 %collective-permute-start.3 = (f32[1,1,32,256]{3,2,1,0:T(8,128)S(1)}, f32[1,1,32,256]{3,2,1,0:T(8,128)S(1)}, u32[]{:S(2)}, u32[]{:S(2)}) collective-permute-start(f32[1,1,32,256]{3,2,1,0:T(8,128)S(1)} %get-tuple-element.656), channel_id=1, source_target_pairs={{0,1},{1,2},{2,3},{3,4},{4,5},{5,6},{6,7},{8,9},{9,10},{10,11},{11... | collective-permute-start | bytes 98312 | tf_op jit(solution)/shard_map/while/body/eval_jaxpr/ppermute | solution.py:19
  64.9 5.8 %collective-permute-start.5 = (f32[1,1,32,256]{3,2,1,0:T(8,128)S(1)}, f32[1,1,32,256]{3,2,1,0:T(8,128)S(1)}, u32[]{:S(2)}, u32[]{:S(2)}) collective-permute-start(f32[1,1,32,256]{3,2,1,0:T(8,128)S(1)} %get-tuple-element.658), channel_id=1, source_target_pairs={{0,1},{1,2},{2,3},{3,4},{4,5},{5,6},{6,7},{8,9},{9,10},{10,11},{11... | collective-permute-start | bytes 98312 | tf_op jit(solution)/shard_map/while/body/eval_jaxpr/ppermute | solution.py:19
  75.9 5.8 %collective-permute-start.7 = (f32[2,1,1,32,256]{4,3,2,1,0:T(8,128)S(1)}, f32[2,1,1,32,256]{4,3,2,1,0:T(8,128)S(1)}, u32[]{:S(2)}, u32[]{:S(2)}) collective-permute-start(f32[2,1,1,32,256]{4,3,2,1,0:T(8,128)S(1)} %get-tuple-element.662), channel_id=1, source_target_pairs={{0,1},{1,2},{2,3},{3,4},{4,5},{5,6},{6,7},{8,9},{9,10},{10,11},{11... | collective-permute-start | bytes 196616 | tf_op jit(solution)/shard_map/while/body/eval_jaxpr/ppermute | solution.py:19
  88.9 5.8 %collective-permute-start.1 = (f32[2,1,1,32,256]{4,3,2,1,0:T(8,128)S(1)}, f32[2,1,1,32,256]{4,3,2,1,0:T(8,128)S(1)}, u32[]{:S(2)}, u32[]{:S(2)}) collective-permute-start(f32[2,1,1,32,256]{4,3,2,1,0:T(8,128)S(1)} %get-tuple-element.644), channel_id=1, source_target_pairs={{0,1},{1,2},{2,3},{3,4},{4,5},{5,6},{6,7},{8,9},{9,10},{10,11},{11... | collective-permute-start | bytes 196616 | tf_op jit(solution)/shard_map/while/body/eval_jaxpr/ppermute | solution.py:19
  99.3 5.4 %collective-permute-start.3 = (f32[1,1,32,256]{3,2,1,0:T(8,128)S(1)}, f32[1,1,32,256]{3,2,1,0:T(8,128)S(1)}, u32[]{:S(2)}, u32[]{:S(2)}) collective-permute-start(f32[1,1,32,256]{3,2,1,0:T(8,128)S(1)} %get-tuple-element.656), channel_id=1, source_target_pairs={{0,1},{1,2},{2,3},{3,4},{4,5},{5,6},{6,7},{8,9},{9,10},{10,11},{11... | collective-permute-start | bytes 98312 | tf_op jit(solution)/shard_map/while/body/eval_jaxpr/ppermute | solution.py:19
  107.8 5.8 %collective-permute-start.5 = (f32[1,1,32,256]{3,2,1,0:T(8,128)S(1)}, f32[1,1,32,256]{3,2,1,0:T(8,128)S(1)}, u32[]{:S(2)}, u32[]{:S(2)}) collective-permute-start(f32[1,1,32,256]{3,2,1,0:T(8,128)S(1)} %get-tuple-element.658), channel_id=1, source_target_pairs={{0,1},{1,2},{2,3},{3,4},{4,5},{5,6},{6,7},{8,9},{9,10},{10,11},{11... | collective-permute-start | bytes 98312 | tf_op jit(solution)/shard_map/while/body/eval_jaxpr/ppermute | solution.py:19
  118.8 5.8 %collective-permute-start.7 = (f32[2,1,1,32,256]{4,3,2,1,0:T(8,128)S(1)}, f32[2,1,1,32,256]{4,3,2,1,0:T(8,128)S(1)}, u32[]{:S(2)}, u32[]{:S(2)}) collective-permute-start(f32[2,1,1,32,256]{4,3,2,1,0:T(8,128)S(1)} %get-tuple-element.662), channel_id=1, source_target_pairs={{0,1},{1,2},{2,3},{3,4},{4,5},{5,6},{6,7},{8,9},{9,10},{10,11},{11... | collective-permute-start | bytes 196616 | tf_op jit(solution)/shard_map/while/body/eval_jaxpr/ppermute | solution.py:19
  131.8 5.9 %collective-permute-start.1 = (f32[2,1,1,32,256]{4,3,2,1,0:T(8,128)S(1)}, f32[2,1,1,32,256]{4,3,2,1,0:T(8,128)S(1)}, u32[]{:S(2)}, u32[]{:S(2)}) collective-permute-start(f32[2,1,1,32,256]{4,3,2,1,0:T(8,128)S(1)} %get-tuple-element.644), channel_id=1, source_target_pairs={{0,1},{1,2},{2,3},{3,4},{4,5},{5,6},{6,7},{8,9},{9,10},{10,11},{11... | collective-permute-start | bytes 196616 | tf_op jit(solution)/shard_map/while/body/eval_jaxpr/ppermute | solution.py:19
  142.6 5.4 %collective-permute-start.3 = (f32[1,1,32,256]{3,2,1,0:T(8,128)S(1)}, f32[1,1,32,256]{3,2,1,0:T(8,128)S(1)}, u32[]{:S(2)}, u32[]{:S(2)}) collective-permute-start(f32[1,1,32,256]{3,2,1,0:T(8,128)S(1)} %get-tuple-element.656), channel_id=1, source_target_pairs={{0,1},{1,2},{2,3},{3,4},{4,5},{5,6},{6,7},{8,9},{9,10},{10,11},{11... | collective-permute-start | bytes 98312 | tf_op jit(solution)/shard_map/while/body/eval_jaxpr/ppermute | solution.py:19
  151.0 5.9 %collective-permute-start.5 = (f32[1,1,32,256]{3,2,1,0:T(8,128)S(1)}, f32[1,1,32,256]{3,2,1,0:T(8,128)S(1)}, u32[]{:S(2)}, u32[]{:S(2)}) collective-permute-start(f32[1,1,32,256]{3,2,1,0:T(8,128)S(1)} %get-tuple-element.658), channel_id=1, source_target_pairs={{0,1},{1,2},{2,3},{3,4},{4,5},{5,6},{6,7},{8,9},{9,10},{10,11},{11... | collective-permute-start | bytes 98312 | tf_op jit(solution)/shard_map/while/body/eval_jaxpr/ppermute | solution.py:19
  162.2 5.7 %collective-permute-start.7 = (f32[2,1,1,32,256]{4,3,2,1,0:T(8,128)S(1)}, f32[2,1,1,32,256]{4,3,2,1,0:T(8,128)S(1)}, u32[]{:S(2)}, u32[]{:S(2)}) collective-permute-start(f32[2,1,1,32,256]{4,3,2,1,0:T(8,128)S(1)} %get-tuple-element.662), channel_id=1, source_target_pairs={{0,1},{1,2},{2,3},{3,4},{4,5},{5,6},{6,7},{8,9},{9,10},{10,11},{11... | collective-permute-start | bytes 196616 | tf_op jit(solution)/shard_map/while/body/eval_jaxpr/ppermute | solution.py:19
  175.2 5.8 %collective-permute-start.1 = (f32[2,1,1,32,256]{4,3,2,1,0:T(8,128)S(1)}, f32[2,1,1,32,256]{4,3,2,1,0:T(8,128)S(1)}, u32[]{:S(2)}, u32[]{:S(2)}) collective-permute-start(f32[2,1,1,32,256]{4,3,2,1,0:T(8,128)S(1)} %get-tuple-element.644), channel_id=1, source_target_pairs={{0,1},{1,2},{2,3},{3,4},{4,5},{5,6},{6,7},{8,9},{9,10},{10,11},{11... | collective-permute-start | bytes 196616 | tf_op jit(solution)/shard_map/while/body/eval_jaxpr/ppermute | solution.py:19
  185.6 5.4 %collective-permute-start.3 = (f32[1,1,32,256]{3,2,1,0:T(8,128)S(1)}, f32[1,1,32,256]{3,2,1,0:T(8,128)S(1)}, u32[]{:S(2)}, u32[]{:S(2)}) collective-permute-start(f32[1,1,32,256]{3,2,1,0:T(8,128)S(1)} %get-tuple-element.656), channel_id=1, source_target_pairs={{0,1},{1,2},{2,3},{3,4},{4,5},{5,6},{6,7},{8,9},{9,10},{10,11},{11... | collective-permute-start | bytes 98312 | tf_op jit(solution)/shard_map/while/body/eval_jaxpr/ppermute | solution.py:19
  194.1 5.8 %collective-permute-start.5 = (f32[1,1,32,256]{3,2,1,0:T(8,128)S(1)}, f32[1,1,32,256]{3,2,1,0:T(8,128)S(1)}, u32[]{:S(2)}, u32[]{:S(2)}) collective-permute-start(f32[1,1,32,256]{3,2,1,0:T(8,128)S(1)} %get-tuple-element.658), channel_id=1, source_target_pairs={{0,1},{1,2},{2,3},{3,4},{4,5},{5,6},{6,7},{8,9},{9,10},{10,11},{11... | collective-permute-start | bytes 98312 | tf_op jit(solution)/shard_map/while/body/eval_jaxpr/ppermute | solution.py:19
  205.1 5.8 %collective-permute-start.7 = (f32[2,1,1,32,256]{4,3,2,1,0:T(8,128)S(1)}, f32[2,1,1,32,256]{4,3,2,1,0:T(8,128)S(1)}, u32[]{:S(2)}, u32[]{:S(2)}) collective-permute-start(f32[2,1,1,32,256]{4,3,2,1,0:T(8,128)S(1)} %get-tuple-element.662), channel_id=1, source_target_pairs={{0,1},{1,2},{2,3},{3,4},{4,5},{5,6},{6,7},{8,9},{9,10},{10,11},{11... | collective-permute-start | bytes 196616 | tf_op jit(solution)/shard_map/while/body/eval_jaxpr/ppermute | solution.py:19
  216.8 12.3 %all_to_all.36 = f32[4,1,4,32,256]{4,3,2,1,0:T(8,128)S(1)} all-to-all(f32[4,1,4,32,256]{4,3,2,1,0:T(8,128)} %get-tuple-element.380), channel_id=1, replica_groups=mesh['tm'=4,'space'=8] {'tm'}, dimensions={0} | all-to-all | bytes 1048576 | tf_op jit(solution)/shard_map/all_to_all | solution.py:189
  232.6 46.4 %psum.7 = f32[4]{0:T(128)S(1)} all-reduce(f32[4]{0:T(128)S(1)} %dynamic_update_slice.24), channel_id=1, replica_groups=mesh['tm'=4,'space'=8] {'tm','space'}, use_global_device_ids=true, to_apply=%region_4.5 | all-reduce | flops 4 | bytes 32 | tf_op jit(solution)/shard_map/psum | solution.py:193
  (189 shorter events, 97.1 us)
Async XLA Ops:
  0.7 44.4 %all-to-all-start = ((f32[4,1,32]{2,1,0:T(1,128)}), f32[4,1,32]{2,1,0:T(1,128)S(1)}, u32[]{:S(2)}, u32[]{:S(2)}) async-start(f32[4,1,32]{2,1,0:T(1,128)} %param.21), calls=%async_computation | async-start | bytes 4096 | tf_op jit(solution)/shard_map/all_to_all | solution.py:159
  63.6 7.1 %collective-permute-start.4 = (f32[1,1,32,256]{3,2,1,0:T(8,128)S(1)}, f32[1,1,32,256]{3,2,1,0:T(8,128)S(1)}, u32[]{:S(2)}, u32[]{:S(2)}) collective-permute-start(f32[1,1,32,256]{3,2,1,0:T(8,128)S(1)} %get-tuple-element.657), channel_id=1, source_target_pairs={{1,0},{2,1},{3,2},{4,3},{5,4},{6,5},{7,6},{9,8},{10,9},{11,10},{12... | collective-permute-start | bytes 98312 | tf_op jit(solution)/shard_map/while/body/eval_jaxpr/ppermute | solution.py:21
  64.9 7.4 %collective-permute-start.5 = (f32[1,1,32,256]{3,2,1,0:T(8,128)S(1)}, f32[1,1,32,256]{3,2,1,0:T(8,128)S(1)}, u32[]{:S(2)}, u32[]{:S(2)}) collective-permute-start(f32[1,1,32,256]{3,2,1,0:T(8,128)S(1)} %get-tuple-element.658), channel_id=1, source_target_pairs={{0,1},{1,2},{2,3},{3,4},{4,5},{5,6},{6,7},{8,9},{9,10},{10,11},{11... | collective-permute-start | bytes 98312 | tf_op jit(solution)/shard_map/while/body/eval_jaxpr/ppermute | solution.py:19
  74.4 12.0 %collective-permute-start.6 = (f32[2,1,1,32,256]{4,3,2,1,0:T(8,128)S(1)}, f32[2,1,1,32,256]{4,3,2,1,0:T(8,128)S(1)}, u32[]{:S(2)}, u32[]{:S(2)}) collective-permute-start(f32[2,1,1,32,256]{4,3,2,1,0:T(8,128)S(1)} %get-tuple-element.661), channel_id=1, source_target_pairs={{1,0},{2,1},{3,2},{4,3},{5,4},{6,5},{7,6},{9,8},{10,9},{11,10},{12... | collective-permute-start | bytes 196616 | tf_op jit(solution)/shard_map/while/body/eval_jaxpr/ppermute | solution.py:21
  75.9 10.6 %collective-permute-start.7 = (f32[2,1,1,32,256]{4,3,2,1,0:T(8,128)S(1)}, f32[2,1,1,32,256]{4,3,2,1,0:T(8,128)S(1)}, u32[]{:S(2)}, u32[]{:S(2)}) collective-permute-start(f32[2,1,1,32,256]{4,3,2,1,0:T(8,128)S(1)} %get-tuple-element.662), channel_id=1, source_target_pairs={{0,1},{1,2},{2,3},{3,4},{4,5},{5,6},{6,7},{8,9},{9,10},{10,11},{11... | collective-permute-start | bytes 196616 | tf_op jit(solution)/shard_map/while/body/eval_jaxpr/ppermute | solution.py:19
  87.6 7.4 %collective-permute-start = (f32[2,1,1,32,256]{4,3,2,1,0:T(8,128)S(1)}, f32[2,1,1,32,256]{4,3,2,1,0:T(8,128)S(1)}, u32[]{:S(2)}, u32[]{:S(2)}) collective-permute-start(f32[2,1,1,32,256]{4,3,2,1,0:T(8,128)S(1)} %get-tuple-element.643), channel_id=1, source_target_pairs={{1,0},{2,1},{3,2},{4,3},{5,4},{6,5},{7,6},{9,8},{10,9},{11,10},{12... | collective-permute-start | bytes 196616 | tf_op jit(solution)/shard_map/while/body/eval_jaxpr/ppermute | solution.py:21
  88.9 7.6 %collective-permute-start.1 = (f32[2,1,1,32,256]{4,3,2,1,0:T(8,128)S(1)}, f32[2,1,1,32,256]{4,3,2,1,0:T(8,128)S(1)}, u32[]{:S(2)}, u32[]{:S(2)}) collective-permute-start(f32[2,1,1,32,256]{4,3,2,1,0:T(8,128)S(1)} %get-tuple-element.644), channel_id=1, source_target_pairs={{0,1},{1,2},{2,3},{3,4},{4,5},{5,6},{6,7},{8,9},{9,10},{10,11},{11... | collective-permute-start | bytes 196616 | tf_op jit(solution)/shard_map/while/body/eval_jaxpr/ppermute | solution.py:19
  106.5 7.1 %collective-permute-start.4 = (f32[1,1,32,256]{3,2,1,0:T(8,128)S(1)}, f32[1,1,32,256]{3,2,1,0:T(8,128)S(1)}, u32[]{:S(2)}, u32[]{:S(2)}) collective-permute-start(f32[1,1,32,256]{3,2,1,0:T(8,128)S(1)} %get-tuple-element.657), channel_id=1, source_target_pairs={{1,0},{2,1},{3,2},{4,3},{5,4},{6,5},{7,6},{9,8},{10,9},{11,10},{12... | collective-permute-start | bytes 98312 | tf_op jit(solution)/shard_map/while/body/eval_jaxpr/ppermute | solution.py:21
  107.8 7.4 %collective-permute-start.5 = (f32[1,1,32,256]{3,2,1,0:T(8,128)S(1)}, f32[1,1,32,256]{3,2,1,0:T(8,128)S(1)}, u32[]{:S(2)}, u32[]{:S(2)}) collective-permute-start(f32[1,1,32,256]{3,2,1,0:T(8,128)S(1)} %get-tuple-element.658), channel_id=1, source_target_pairs={{0,1},{1,2},{2,3},{3,4},{4,5},{5,6},{6,7},{8,9},{9,10},{10,11},{11... | collective-permute-start | bytes 98312 | tf_op jit(solution)/shard_map/while/body/eval_jaxpr/ppermute | solution.py:19
  117.4 12.0 %collective-permute-start.6 = (f32[2,1,1,32,256]{4,3,2,1,0:T(8,128)S(1)}, f32[2,1,1,32,256]{4,3,2,1,0:T(8,128)S(1)}, u32[]{:S(2)}, u32[]{:S(2)}) collective-permute-start(f32[2,1,1,32,256]{4,3,2,1,0:T(8,128)S(1)} %get-tuple-element.661), channel_id=1, source_target_pairs={{1,0},{2,1},{3,2},{4,3},{5,4},{6,5},{7,6},{9,8},{10,9},{11,10},{12... | collective-permute-start | bytes 196616 | tf_op jit(solution)/shard_map/while/body/eval_jaxpr/ppermute | solution.py:21
  118.8 10.6 %collective-permute-start.7 = (f32[2,1,1,32,256]{4,3,2,1,0:T(8,128)S(1)}, f32[2,1,1,32,256]{4,3,2,1,0:T(8,128)S(1)}, u32[]{:S(2)}, u32[]{:S(2)}) collective-permute-start(f32[2,1,1,32,256]{4,3,2,1,0:T(8,128)S(1)} %get-tuple-element.662), channel_id=1, source_target_pairs={{0,1},{1,2},{2,3},{3,4},{4,5},{5,6},{6,7},{8,9},{9,10},{10,11},{11... | collective-permute-start | bytes 196616 | tf_op jit(solution)/shard_map/while/body/eval_jaxpr/ppermute | solution.py:19
  130.5 7.6 %collective-permute-start = (f32[2,1,1,32,256]{4,3,2,1,0:T(8,128)S(1)}, f32[2,1,1,32,256]{4,3,2,1,0:T(8,128)S(1)}, u32[]{:S(2)}, u32[]{:S(2)}) collective-permute-start(f32[2,1,1,32,256]{4,3,2,1,0:T(8,128)S(1)} %get-tuple-element.643), channel_id=1, source_target_pairs={{1,0},{2,1},{3,2},{4,3},{5,4},{6,5},{7,6},{9,8},{10,9},{11,10},{12... | collective-permute-start | bytes 196616 | tf_op jit(solution)/shard_map/while/body/eval_jaxpr/ppermute | solution.py:21
  131.8 8.0 %collective-permute-start.1 = (f32[2,1,1,32,256]{4,3,2,1,0:T(8,128)S(1)}, f32[2,1,1,32,256]{4,3,2,1,0:T(8,128)S(1)}, u32[]{:S(2)}, u32[]{:S(2)}) collective-permute-start(f32[2,1,1,32,256]{4,3,2,1,0:T(8,128)S(1)} %get-tuple-element.644), channel_id=1, source_target_pairs={{0,1},{1,2},{2,3},{3,4},{4,5},{5,6},{6,7},{8,9},{9,10},{10,11},{11... | collective-permute-start | bytes 196616 | tf_op jit(solution)/shard_map/while/body/eval_jaxpr/ppermute | solution.py:19
  149.7 7.3 %collective-permute-start.4 = (f32[1,1,32,256]{3,2,1,0:T(8,128)S(1)}, f32[1,1,32,256]{3,2,1,0:T(8,128)S(1)}, u32[]{:S(2)}, u32[]{:S(2)}) collective-permute-start(f32[1,1,32,256]{3,2,1,0:T(8,128)S(1)} %get-tuple-element.657), channel_id=1, source_target_pairs={{1,0},{2,1},{3,2},{4,3},{5,4},{6,5},{7,6},{9,8},{10,9},{11,10},{12... | collective-permute-start | bytes 98312 | tf_op jit(solution)/shard_map/while/body/eval_jaxpr/ppermute | solution.py:21
  151.0 7.6 %collective-permute-start.5 = (f32[1,1,32,256]{3,2,1,0:T(8,128)S(1)}, f32[1,1,32,256]{3,2,1,0:T(8,128)S(1)}, u32[]{:S(2)}, u32[]{:S(2)}) collective-permute-start(f32[1,1,32,256]{3,2,1,0:T(8,128)S(1)} %get-tuple-element.658), channel_id=1, source_target_pairs={{0,1},{1,2},{2,3},{3,4},{4,5},{5,6},{6,7},{8,9},{9,10},{10,11},{11... | collective-permute-start | bytes 98312 | tf_op jit(solution)/shard_map/while/body/eval_jaxpr/ppermute | solution.py:19
  160.8 12.0 %collective-permute-start.6 = (f32[2,1,1,32,256]{4,3,2,1,0:T(8,128)S(1)}, f32[2,1,1,32,256]{4,3,2,1,0:T(8,128)S(1)}, u32[]{:S(2)}, u32[]{:S(2)}) collective-permute-start(f32[2,1,1,32,256]{4,3,2,1,0:T(8,128)S(1)} %get-tuple-element.661), channel_id=1, source_target_pairs={{1,0},{2,1},{3,2},{4,3},{5,4},{6,5},{7,6},{9,8},{10,9},{11,10},{12... | collective-permute-start | bytes 196616 | tf_op jit(solution)/shard_map/while/body/eval_jaxpr/ppermute | solution.py:21
  162.2 10.5 %collective-permute-start.7 = (f32[2,1,1,32,256]{4,3,2,1,0:T(8,128)S(1)}, f32[2,1,1,32,256]{4,3,2,1,0:T(8,128)S(1)}, u32[]{:S(2)}, u32[]{:S(2)}) collective-permute-start(f32[2,1,1,32,256]{4,3,2,1,0:T(8,128)S(1)} %get-tuple-element.662), channel_id=1, source_target_pairs={{0,1},{1,2},{2,3},{3,4},{4,5},{5,6},{6,7},{8,9},{9,10},{10,11},{11... | collective-permute-start | bytes 196616 | tf_op jit(solution)/shard_map/while/body/eval_jaxpr/ppermute | solution.py:19
  173.9 7.4 %collective-permute-start = (f32[2,1,1,32,256]{4,3,2,1,0:T(8,128)S(1)}, f32[2,1,1,32,256]{4,3,2,1,0:T(8,128)S(1)}, u32[]{:S(2)}, u32[]{:S(2)}) collective-permute-start(f32[2,1,1,32,256]{4,3,2,1,0:T(8,128)S(1)} %get-tuple-element.643), channel_id=1, source_target_pairs={{1,0},{2,1},{3,2},{4,3},{5,4},{6,5},{7,6},{9,8},{10,9},{11,10},{12... | collective-permute-start | bytes 196616 | tf_op jit(solution)/shard_map/while/body/eval_jaxpr/ppermute | solution.py:21
  175.2 7.6 %collective-permute-start.1 = (f32[2,1,1,32,256]{4,3,2,1,0:T(8,128)S(1)}, f32[2,1,1,32,256]{4,3,2,1,0:T(8,128)S(1)}, u32[]{:S(2)}, u32[]{:S(2)}) collective-permute-start(f32[2,1,1,32,256]{4,3,2,1,0:T(8,128)S(1)} %get-tuple-element.644), channel_id=1, source_target_pairs={{0,1},{1,2},{2,3},{3,4},{4,5},{5,6},{6,7},{8,9},{9,10},{10,11},{11... | collective-permute-start | bytes 196616 | tf_op jit(solution)/shard_map/while/body/eval_jaxpr/ppermute | solution.py:19
  192.8 7.1 %collective-permute-start.4 = (f32[1,1,32,256]{3,2,1,0:T(8,128)S(1)}, f32[1,1,32,256]{3,2,1,0:T(8,128)S(1)}, u32[]{:S(2)}, u32[]{:S(2)}) collective-permute-start(f32[1,1,32,256]{3,2,1,0:T(8,128)S(1)} %get-tuple-element.657), channel_id=1, source_target_pairs={{1,0},{2,1},{3,2},{4,3},{5,4},{6,5},{7,6},{9,8},{10,9},{11,10},{12... | collective-permute-start | bytes 98312 | tf_op jit(solution)/shard_map/while/body/eval_jaxpr/ppermute | solution.py:21
  194.1 7.4 %collective-permute-start.5 = (f32[1,1,32,256]{3,2,1,0:T(8,128)S(1)}, f32[1,1,32,256]{3,2,1,0:T(8,128)S(1)}, u32[]{:S(2)}, u32[]{:S(2)}) collective-permute-start(f32[1,1,32,256]{3,2,1,0:T(8,128)S(1)} %get-tuple-element.658), channel_id=1, source_target_pairs={{0,1},{1,2},{2,3},{3,4},{4,5},{5,6},{6,7},{8,9},{9,10},{10,11},{11... | collective-permute-start | bytes 98312 | tf_op jit(solution)/shard_map/while/body/eval_jaxpr/ppermute | solution.py:19
  203.7 12.0 %collective-permute-start.6 = (f32[2,1,1,32,256]{4,3,2,1,0:T(8,128)S(1)}, f32[2,1,1,32,256]{4,3,2,1,0:T(8,128)S(1)}, u32[]{:S(2)}, u32[]{:S(2)}) collective-permute-start(f32[2,1,1,32,256]{4,3,2,1,0:T(8,128)S(1)} %get-tuple-element.661), channel_id=1, source_target_pairs={{1,0},{2,1},{3,2},{4,3},{5,4},{6,5},{7,6},{9,8},{10,9},{11,10},{12... | collective-permute-start | bytes 196616 | tf_op jit(solution)/shard_map/while/body/eval_jaxpr/ppermute | solution.py:21
  205.1 10.6 %collective-permute-start.7 = (f32[2,1,1,32,256]{4,3,2,1,0:T(8,128)S(1)}, f32[2,1,1,32,256]{4,3,2,1,0:T(8,128)S(1)}, u32[]{:S(2)}, u32[]{:S(2)}) collective-permute-start(f32[2,1,1,32,256]{4,3,2,1,0:T(8,128)S(1)} %get-tuple-element.662), channel_id=1, source_target_pairs={{0,1},{1,2},{2,3},{3,4},{4,5},{5,6},{6,7},{8,9},{9,10},{10,11},{11... | collective-permute-start | bytes 196616 | tf_op jit(solution)/shard_map/while/body/eval_jaxpr/ppermute | solution.py:19
  229.0 50.5 %all-to-all-start.2 = ((f32[4,1,4,32,256]{4,3,2,1,0:T(8,128)}), f32[4,1,4,32,256]{4,3,2,1,0:T(8,128)S(1)}, u32[]{:S(2)}, u32[]{:S(2)}) async-start(f32[4,1,4,32,256]{4,3,2,1,0:T(8,128)} %get-tuple-element.381), calls=%async_computation.2 | async-start | bytes 1048576 | tf_op jit(solution)/shard_map/all_to_all | solution.py:190
  (32 other events, 182.1 us)
where the time goes:
time: 283 us; the launch traced here: 281 us
  starting transfers between devices  119 us (42%)
  blocking collectives  79.4 us (28%)
  other arithmetic  33.1 us (12%)
  waiting for transfers between devices  20.6 us (7%)
  matrix products  17.5 us (6%)
  local copies, waits for them, and re-layouts  7.58 us (3%)
  loops' own time  3.42 us (1%)
    ppermute x16, starting transfers between devices, padded(): lax.ppermute(tail, axis, [(i, (i + 1) % count) for i in range(ends)])  89.6 us
    psum x1, blocking collectives, body(): totals = lax.psum(misfit, ('tm', 'space'))  46.4 us
    ppermute x16, starting transfers between devices, padded(): lax.ppermute(head, axis, [((i + 1) % count, i) for i in range(ends)])  21.2 us
    ppermute x16, waiting for transfers between devices, padded(): lax.ppermute(tail, axis, [(i, (i + 1) % count) for i in range(ends)])  18.9 us
    dot_general x4, matrix products, mismatch(): jnp.dot(pressure.reshape(batch_size, -1), well_picks.T, precision=lax.Pre...  16.2 us
    all_to_all x1, blocking collectives, body(): lax.all_to_all(result[2], 'tm', split_axis=0, concat_axis=1, tiled=True)  12.3 us
    add x2, other arithmetic, region_fields(): summed + jnp.where(region_ids == region_index, region_table[table_row, re...  10.3 us
    all_gather x1, blocking collectives, body(): lax.all_gather(inflow, 'tm', axis=0, tiled=True)  8.19 us
  transfers between devices with their start and end apart: 34, of which 17 were waited for; matrix products, arithmetic and copies ran while one was open for 13% of the time, Pallas kernels for 0%

commit v1 on v0

--- a/solution.py
+++ b/solution.py
@@ -190,7 +190,8 @@
         lax.all_to_all(result[3], "tm", split_axis=0, concat_axis=1, tiled=True),
     )
     misfit = lax.dynamic_update_slice_in_dim(misfit, result[4], section_index * batch_size, 0)
-    totals = lax.psum(misfit, ("tm", "space"))
+    parts = lax.all_gather(misfit, ("tm", "space"), axis=0, tiled=False)
+    totals = parts.sum(axis=0)
     return (totals / (sections * REP_DEV * well_cells.shape[0]), slab_pressure, slab_saturation)
 
 

time: 283 us -> 308 us (1.088)
  blocking collectives: 79.4 us -> 104 us
    all_gather x0 -> x1, blocking collectives: none -> 71.4 us  [body(): parts = lax.all_gather(misfit, ('tm', 'space'), axis=0, tiled=False)]
    psum x1 -> x0, blocking collectives: 46.4 us -> none  [body(): totals = lax.psum(misfit, ('tm', 'space'))]
  transfers between devices with their start and end apart: 34 -> 34, of which waited for: 17 -> 17; matrix products, arithmetic and copies ran while one was open for 13% -> 12% of each run, Pallas kernels for 0% -> 0%
where the time goes in v1:
time: 308 us; the launch traced here: 306 us
  starting transfers between devices  119 us (39%)
  blocking collectives  104 us (34%)
  other arithmetic  33.2 us (11%)
  waiting for transfers between devices  20.6 us (7%)
  matrix products  17.5 us (6%)
  local copies, waits for them, and re-layouts  7.51 us (2%)
  loops' own time  3.42 us (1%)
    ppermute x16, starting transfers between devices, padded(): lax.ppermute(tail, axis, [(i, (i + 1) % count) for i in range(ends)])  89.6 us
    all_gather x1, blocking collectives, body(): parts = lax.all_gather(misfit, ('tm', 'space'), axis=0, tiled=False)  71.4 us
    ppermute x16, starting transfers between devices, padded(): lax.ppermute(head, axis, [((i + 1) % count, i) for i in range(ends)])  21.2 us
    ppermute x16, waiting for transfers between devices, padded(): lax.ppermute(tail, axis, [(i, (i + 1) % count) for i in range(ends)])  18.9 us
    dot_general x4, matrix products, mismatch(): jnp.dot(pressure.reshape(batch_size, -1), well_picks.T, precision=lax.Pre...  16.2 us
    all_to_all x1, blocking collectives, body(): lax.all_to_all(result[2], 'tm', split_axis=0, concat_axis=1, tiled=True)  12.3 us
    add x2, other arithmetic, region_fields(): summed + jnp.where(region_ids == region_index, region_table[table_row, re...  10.3 us
    all_gather x1, blocking collectives, body(): lax.all_gather(inflow, 'tm', axis=0, tiled=True)  8.19 us
  transfers between devices with their start and end apart: 34, of which 17 were waited for; matrix products, arithmetic and copies ran while one was open for 12% of the time, Pallas kernels for 0%

profile of v1, /device:TPU:0, one launch (start us, length us, event | category | flops | bytes accessed | tf_op | source)
XLA Modules:
  0.0 306.1 jit_solution(3747747486979522698)
XLA Ops:
  6.7 5.2 %all-gather = f32[4,1,32]{2,1,0:T(1,128)S(1)} all-gather(f32[1,1,32]{2,1,0:T(1,128)S(1)} %bitcast.155), channel_id=1, replica_groups=mesh['tm'=4,'space'=8] {'tm'}, dimensions={0}, use_global_device_ids=true | all-gather | bytes 640 | tf_op jit(solution)/shard_map/all_gather | solution.py:157
  13.9 8.2 %all_gather.19 = f32[4,4,32,256]{3,2,1,0:T(8,128)} all-gather(f32[1,4,32,256]{3,2,1,0:T(8,128)S(1)} %copy-done.7), channel_id=1, replica_groups=mesh['tm'=4,'space'=8] {'tm'}, dimensions={0}, use_global_device_ids=true | all-gather | bytes 655360 | tf_op jit(solution)/shard_map/all_gather | solution.py:156
  22.1 7.4 %all_gather.20 = f32[4,4,32,256]{3,2,1,0:T(8,128)S(1)} all-gather(f32[1,4,32,256]{3,2,1,0:T(8,128)S(1)} %copy-done.8), channel_id=1, replica_groups=mesh['tm'=4,'space'=8] {'tm'}, dimensions={0}, use_global_device_ids=true | all-gather | bytes 655360 | tf_op jit(solution)/shard_map/all_gather | solution.py:155
  29.6 5.2 %select_add_fusion = (f32[4,32,256]{2,1,0:T(8,128)S(1)}, pred[4,32,256]{2,1,0:T(8,128)(4,1)S(1)}, pred[4,32,256]{2,1,0:T(8,128)(4,1)S(1)}, pred[4,32,256]{2,1,0:...) fusion(f32[]{:T(128)} %bitcast.28, f32[]{:T(128)} %bitcast.27, ...), kind=kLoop, calls=%fused_computation.152 | loop fusion | flops 753664 | bytes 524320 | tf_op jit(solution)/shard_map/add | solution.py:96
  34.8 5.1 %add_multiply_fusion = f32[4,32,256]{2,1,0:T(8,128)S(1)} fusion(pred[4,32,256]{2,1,0:T(8,128)(4,1)S(1)} %get-tuple-element.474, pred[4,32,256]{2,1,0:T(8,128)(4,1)S(1)} %get-tuple-element.473, pred[4,32,256]{2,1,0:T(8,128)(4,1)S(1)} %get-tuple-element.472, pred[4,32,256]{2,1,0:T(8,128)(4,1)S(1)} %get-tuple-element.471, ...), kind=kLoop, calls=%fused_computation.153 | loop fusion | flops 524288 | bytes 393248 | tf_op jit(solution)/shard_map/mul | solution.py:100
  39.8 5.1 %select_add_fusion.1 = f32[4,32,256]{2,1,0:T(8,128)S(1)} fusion(pred[4,32,256]{2,1,0:T(8,128)(4,1)S(1)} %get-tuple-element.474, pred[4,32,256]{2,1,0:T(8,128)(4,1)S(1)} %get-tuple-element.473, pred[4,32,256]{2,1,0:T(8,128)(4,1)S(1)} %get-tuple-element.472, pred[4,32,256]{2,1,0:T(8,128)(4,1)S(1)} %get-tuple-element.471, ...), kind=kLoop, calls=%fused_computation.155 | loop fusion | flops 491520 | bytes 393248 | tf_op jit(solution)/shard_map/add | solution.py:96
  46.0 170.8 %while.24 = (s32[]{:T(128)}, f32[1,4,32,256]{3,2,1,0:T(8,128)S(1)}, f32[1,4,32,256]{3,2,1,0:T(8,128)S(1)}, f32[4,1,4,32,256]{4,3,2,1,0:T(8,128)}, f32[4,1,4,32,2...) while((s32[]{:T(128)}, f32[1,4,32,256]{3,2,1,0:T(8,128)S(1)}, ...), condition=%wide.region_3.4_spmd.clone, body=%wide.region_1.3_spmd.clone.sunk | while | flops 19529856 | bytes 16516069 | solution.py:182
  56.7 5.1 %collective-permute-start.3 = (f32[1,1,32,256]{3,2,1,0:T(8,128)S(1)}, f32[1,1,32,256]{3,2,1,0:T(8,128)S(1)}, u32[]{:S(2)}, u32[]{:S(2)}) collective-permute-start(f32[1,1,32,256]{3,2,1,0:T(8,128)S(1)} %get-tuple-element.656), channel_id=1, source_target_pairs={{0,1},{1,2},{2,3},{3,4},{4,5},{5,6},{6,7},{8,9},{9,10},{10,11},{11... | collective-permute-start | bytes 98312 | tf_op jit(solution)/shard_map/while/body/eval_jaxpr/ppermute | solution.py:19
  64.9 5.8 %collective-permute-start.5 = (f32[1,1,32,256]{3,2,1,0:T(8,128)S(1)}, f32[1,1,32,256]{3,2,1,0:T(8,128)S(1)}, u32[]{:S(2)}, u32[]{:S(2)}) collective-permute-start(f32[1,1,32,256]{3,2,1,0:T(8,128)S(1)} %get-tuple-element.658), channel_id=1, source_target_pairs={{0,1},{1,2},{2,3},{3,4},{4,5},{5,6},{6,7},{8,9},{9,10},{10,11},{11... | collective-permute-start | bytes 98312 | tf_op jit(solution)/shard_map/while/body/eval_jaxpr/ppermute | solution.py:19
  75.9 5.8 %collective-permute-start.7 = (f32[2,1,1,32,256]{4,3,2,1,0:T(8,128)S(1)}, f32[2,1,1,32,256]{4,3,2,1,0:T(8,128)S(1)}, u32[]{:S(2)}, u32[]{:S(2)}) collective-permute-start(f32[2,1,1,32,256]{4,3,2,1,0:T(8,128)S(1)} %get-tuple-element.662), channel_id=1, source_target_pairs={{0,1},{1,2},{2,3},{3,4},{4,5},{5,6},{6,7},{8,9},{9,10},{10,11},{11... | collective-permute-start | bytes 196616 | tf_op jit(solution)/shard_map/while/body/eval_jaxpr/ppermute | solution.py:19
  88.9 5.8 %collective-permute-start.1 = (f32[2,1,1,32,256]{4,3,2,1,0:T(8,128)S(1)}, f32[2,1,1,32,256]{4,3,2,1,0:T(8,128)S(1)}, u32[]{:S(2)}, u32[]{:S(2)}) collective-permute-start(f32[2,1,1,32,256]{4,3,2,1,0:T(8,128)S(1)} %get-tuple-element.644), channel_id=1, source_target_pairs={{0,1},{1,2},{2,3},{3,4},{4,5},{5,6},{6,7},{8,9},{9,10},{10,11},{11... | collective-permute-start | bytes 196616 | tf_op jit(solution)/shard_map/while/body/eval_jaxpr/ppermute | solution.py:19
  99.3 5.4 %collective-permute-start.3 = (f32[1,1,32,256]{3,2,1,0:T(8,128)S(1)}, f32[1,1,32,256]{3,2,1,0:T(8,128)S(1)}, u32[]{:S(2)}, u32[]{:S(2)}) collective-permute-start(f32[1,1,32,256]{3,2,1,0:T(8,128)S(1)} %get-tuple-element.656), channel_id=1, source_target_pairs={{0,1},{1,2},{2,3},{3,4},{4,5},{5,6},{6,7},{8,9},{9,10},{10,11},{11... | collective-permute-start | bytes 98312 | tf_op jit(solution)/shard_map/while/body/eval_jaxpr/ppermute | solution.py:19
  107.8 5.8 %collective-permute-start.5 = (f32[1,1,32,256]{3,2,1,0:T(8,128)S(1)}, f32[1,1,32,256]{3,2,1,0:T(8,128)S(1)}, u32[]{:S(2)}, u32[]{:S(2)}) collective-permute-start(f32[1,1,32,256]{3,2,1,0:T(8,128)S(1)} %get-tuple-element.658), channel_id=1, source_target_pairs={{0,1},{1,2},{2,3},{3,4},{4,5},{5,6},{6,7},{8,9},{9,10},{10,11},{11... | collective-permute-start | bytes 98312 | tf_op jit(solution)/shard_map/while/body/eval_jaxpr/ppermute | solution.py:19
  118.8 5.8 %collective-permute-start.7 = (f32[2,1,1,32,256]{4,3,2,1,0:T(8,128)S(1)}, f32[2,1,1,32,256]{4,3,2,1,0:T(8,128)S(1)}, u32[]{:S(2)}, u32[]{:S(2)}) collective-permute-start(f32[2,1,1,32,256]{4,3,2,1,0:T(8,128)S(1)} %get-tuple-element.662), channel_id=1, source_target_pairs={{0,1},{1,2},{2,3},{3,4},{4,5},{5,6},{6,7},{8,9},{9,10},{10,11},{11... | collective-permute-start | bytes 196616 | tf_op jit(solution)/shard_map/while/body/eval_jaxpr/ppermute | solution.py:19
  131.8 5.9 %collective-permute-start.1 = (f32[2,1,1,32,256]{4,3,2,1,0:T(8,128)S(1)}, f32[2,1,1,32,256]{4,3,2,1,0:T(8,128)S(1)}, u32[]{:S(2)}, u32[]{:S(2)}) collective-permute-start(f32[2,1,1,32,256]{4,3,2,1,0:T(8,128)S(1)} %get-tuple-element.644), channel_id=1, source_target_pairs={{0,1},{1,2},{2,3},{3,4},{4,5},{5,6},{6,7},{8,9},{9,10},{10,11},{11... | collective-permute-start | bytes 196616 | tf_op jit(solution)/shard_map/while/body/eval_jaxpr/ppermute | solution.py:19
  142.6 5.4 %collective-permute-start.3 = (f32[1,1,32,256]{3,2,1,0:T(8,128)S(1)}, f32[1,1,32,256]{3,2,1,0:T(8,128)S(1)}, u32[]{:S(2)}, u32[]{:S(2)}) collective-permute-start(f32[1,1,32,256]{3,2,1,0:T(8,128)S(1)} %get-tuple-element.656), channel_id=1, source_target_pairs={{0,1},{1,2},{2,3},{3,4},{4,5},{5,6},{6,7},{8,9},{9,10},{10,11},{11... | collective-permute-start | bytes 98312 | tf_op jit(solution)/shard_map/while/body/eval_jaxpr/ppermute | solution.py:19
  151.0 5.9 %collective-permute-start.5 = (f32[1,1,32,256]{3,2,1,0:T(8,128)S(1)}, f32[1,1,32,256]{3,2,1,0:T(8,128)S(1)}, u32[]{:S(2)}, u32[]{:S(2)}) collective-permute-start(f32[1,1,32,256]{3,2,1,0:T(8,128)S(1)} %get-tuple-element.658), channel_id=1, source_target_pairs={{0,1},{1,2},{2,3},{3,4},{4,5},{5,6},{6,7},{8,9},{9,10},{10,11},{11... | collective-permute-start | bytes 98312 | tf_op jit(solution)/shard_map/while/body/eval_jaxpr/ppermute | solution.py:19
  162.2 5.7 %collective-permute-start.7 = (f32[2,1,1,32,256]{4,3,2,1,0:T(8,128)S(1)}, f32[2,1,1,32,256]{4,3,2,1,0:T(8,128)S(1)}, u32[]{:S(2)}, u32[]{:S(2)}) collective-permute-start(f32[2,1,1,32,256]{4,3,2,1,0:T(8,128)S(1)} %get-tuple-element.662), channel_id=1, source_target_pairs={{0,1},{1,2},{2,3},{3,4},{4,5},{5,6},{6,7},{8,9},{9,10},{10,11},{11... | collective-permute-start | bytes 196616 | tf_op jit(solution)/shard_map/while/body/eval_jaxpr/ppermute | solution.py:19
  175.2 5.8 %collective-permute-start.1 = (f32[2,1,1,32,256]{4,3,2,1,0:T(8,128)S(1)}, f32[2,1,1,32,256]{4,3,2,1,0:T(8,128)S(1)}, u32[]{:S(2)}, u32[]{:S(2)}) collective-permute-start(f32[2,1,1,32,256]{4,3,2,1,0:T(8,128)S(1)} %get-tuple-element.644), channel_id=1, source_target_pairs={{0,1},{1,2},{2,3},{3,4},{4,5},{5,6},{6,7},{8,9},{9,10},{10,11},{11... | collective-permute-start | bytes 196616 | tf_op jit(solution)/shard_map/while/body/eval_jaxpr/ppermute | solution.py:19
  185.6 5.4 %collective-permute-start.3 = (f32[1,1,32,256]{3,2,1,0:T(8,128)S(1)}, f32[1,1,32,256]{3,2,1,0:T(8,128)S(1)}, u32[]{:S(2)}, u32[]{:S(2)}) collective-permute-start(f32[1,1,32,256]{3,2,1,0:T(8,128)S(1)} %get-tuple-element.656), channel_id=1, source_target_pairs={{0,1},{1,2},{2,3},{3,4},{4,5},{5,6},{6,7},{8,9},{9,10},{10,11},{11... | collective-permute-start | bytes 98312 | tf_op jit(solution)/shard_map/while/body/eval_jaxpr/ppermute | solution.py:19
  194.1 5.8 %collective-permute-start.5 = (f32[1,1,32,256]{3,2,1,0:T(8,128)S(1)}, f32[1,1,32,256]{3,2,1,0:T(8,128)S(1)}, u32[]{:S(2)}, u32[]{:S(2)}) collective-permute-start(f32[1,1,32,256]{3,2,1,0:T(8,128)S(1)} %get-tuple-element.658), channel_id=1, source_target_pairs={{0,1},{1,2},{2,3},{3,4},{4,5},{5,6},{6,7},{8,9},{9,10},{10,11},{11... | collective-permute-start | bytes 98312 | tf_op jit(solution)/shard_map/while/body/eval_jaxpr/ppermute | solution.py:19
  205.1 5.8 %collective-permute-start.7 = (f32[2,1,1,32,256]{4,3,2,1,0:T(8,128)S(1)}, f32[2,1,1,32,256]{4,3,2,1,0:T(8,128)S(1)}, u32[]{:S(2)}, u32[]{:S(2)}) collective-permute-start(f32[2,1,1,32,256]{4,3,2,1,0:T(8,128)S(1)} %get-tuple-element.662), channel_id=1, source_target_pairs={{0,1},{1,2},{2,3},{3,4},{4,5},{5,6},{6,7},{8,9},{9,10},{10,11},{11... | collective-permute-start | bytes 196616 | tf_op jit(solution)/shard_map/while/body/eval_jaxpr/ppermute | solution.py:19
  216.8 12.3 %all_to_all.36 = f32[4,1,4,32,256]{4,3,2,1,0:T(8,128)S(1)} all-to-all(f32[4,1,4,32,256]{4,3,2,1,0:T(8,128)} %get-tuple-element.380), channel_id=1, replica_groups=mesh['tm'=4,'space'=8] {'tm'}, dimensions={0} | all-to-all | bytes 1048576 | tf_op jit(solution)/shard_map/all_to_all | solution.py:189
  232.6 71.4 %all-gather.1 = f32[32,1,4]{2,1,0:T(1,128)S(1)} all-gather(f32[1,1,4]{2,1,0:T(1,128)S(1)} %dynamic_update_slice.26), channel_id=1, replica_groups=mesh['tm'=4,'space'=8] {'tm','space'}, dimensions={0}, use_global_device_ids=true | all-gather | bytes 528 | tf_op jit(solution)/shard_map/all_gather | solution.py:193
  (190 shorter events, 97.1 us)
Async XLA Ops:
  0.7 44.4 %all-to-all-start = ((f32[4,1,32]{2,1,0:T(1,128)}), f32[4,1,32]{2,1,0:T(1,128)S(1)}, u32[]{:S(2)}, u32[]{:S(2)}) async-start(f32[4,1,32]{2,1,0:T(1,128)} %param.21), calls=%async_computation | async-start | bytes 4096 | tf_op jit(solution)/shard_map/all_to_all | solution.py:159
  63.6 7.1 %collective-permute-start.4 = (f32[1,1,32,256]{3,2,1,0:T(8,128)S(1)}, f32[1,1,32,256]{3,2,1,0:T(8,128)S(1)}, u32[]{:S(2)}, u32[]{:S(2)}) collective-permute-start(f32[1,1,32,256]{3,2,1,0:T(8,128)S(1)} %get-tuple-element.657), channel_id=1, source_target_pairs={{1,0},{2,1},{3,2},{4,3},{5,4},{6,5},{7,6},{9,8},{10,9},{11,10},{12... | collective-permute-start | bytes 98312 | tf_op jit(solution)/shard_map/while/body/eval_jaxpr/ppermute | solution.py:21
  64.9 7.4 %collective-permute-start.5 = (f32[1,1,32,256]{3,2,1,0:T(8,128)S(1)}, f32[1,1,32,256]{3,2,1,0:T(8,128)S(1)}, u32[]{:S(2)}, u32[]{:S(2)}) collective-permute-start(f32[1,1,32,256]{3,2,1,0:T(8,128)S(1)} %get-tuple-element.658), channel_id=1, source_target_pairs={{0,1},{1,2},{2,3},{3,4},{4,5},{5,6},{6,7},{8,9},{9,10},{10,11},{11... | collective-permute-start | bytes 98312 | tf_op jit(solution)/shard_map/while/body/eval_jaxpr/ppermute | solution.py:19
  74.4 12.0 %collective-permute-start.6 = (f32[2,1,1,32,256]{4,3,2,1,0:T(8,128)S(1)}, f32[2,1,1,32,256]{4,3,2,1,0:T(8,128)S(1)}, u32[]{:S(2)}, u32[]{:S(2)}) collective-permute-start(f32[2,1,1,32,256]{4,3,2,1,0:T(8,128)S(1)} %get-tuple-element.661), channel_id=1, source_target_pairs={{1,0},{2,1},{3,2},{4,3},{5,4},{6,5},{7,6},{9,8},{10,9},{11,10},{12... | collective-permute-start | bytes 196616 | tf_op jit(solution)/shard_map/while/body/eval_jaxpr/ppermute | solution.py:21
  75.9 10.6 %collective-permute-start.7 = (f32[2,1,1,32,256]{4,3,2,1,0:T(8,128)S(1)}, f32[2,1,1,32,256]{4,3,2,1,0:T(8,128)S(1)}, u32[]{:S(2)}, u32[]{:S(2)}) collective-permute-start(f32[2,1,1,32,256]{4,3,2,1,0:T(8,128)S(1)} %get-tuple-element.662), channel_id=1, source_target_pairs={{0,1},{1,2},{2,3},{3,4},{4,5},{5,6},{6,7},{8,9},{9,10},{10,11},{11... | collective-permute-start | bytes 196616 | tf_op jit(solution)/shard_map/while/body/eval_jaxpr/ppermute | solution.py:19
  87.6 7.4 %collective-permute-start = (f32[2,1,1,32,256]{4,3,2,1,0:T(8,128)S(1)}, f32[2,1,1,32,256]{4,3,2,1,0:T(8,128)S(1)}, u32[]{:S(2)}, u32[]{:S(2)}) collective-permute-start(f32[2,1,1,32,256]{4,3,2,1,0:T(8,128)S(1)} %get-tuple-element.643), channel_id=1, source_target_pairs={{1,0},{2,1},{3,2},{4,3},{5,4},{6,5},{7,6},{9,8},{10,9},{11,10},{12... | collective-permute-start | bytes 196616 | tf_op jit(solution)/shard_map/while/body/eval_jaxpr/ppermute | solution.py:21
  88.9 7.6 %collective-permute-start.1 = (f32[2,1,1,32,256]{4,3,2,1,0:T(8,128)S(1)}, f32[2,1,1,32,256]{4,3,2,1,0:T(8,128)S(1)}, u32[]{:S(2)}, u32[]{:S(2)}) collective-permute-start(f32[2,1,1,32,256]{4,3,2,1,0:T(8,128)S(1)} %get-tuple-element.644), channel_id=1, source_target_pairs={{0,1},{1,2},{2,3},{3,4},{4,5},{5,6},{6,7},{8,9},{9,10},{10,11},{11... | collective-permute-start | bytes 196616 | tf_op jit(solution)/shard_map/while/body/eval_jaxpr/ppermute | solution.py:19
  106.5 7.1 %collective-permute-start.4 = (f32[1,1,32,256]{3,2,1,0:T(8,128)S(1)}, f32[1,1,32,256]{3,2,1,0:T(8,128)S(1)}, u32[]{:S(2)}, u32[]{:S(2)}) collective-permute-start(f32[1,1,32,256]{3,2,1,0:T(8,128)S(1)} %get-tuple-element.657), channel_id=1, source_target_pairs={{1,0},{2,1},{3,2},{4,3},{5,4},{6,5},{7,6},{9,8},{10,9},{11,10},{12... | collective-permute-start | bytes 98312 | tf_op jit(solution)/shard_map/while/body/eval_jaxpr/ppermute | solution.py:21
  107.8 7.4 %collective-permute-start.5 = (f32[1,1,32,256]{3,2,1,0:T(8,128)S(1)}, f32[1,1,32,256]{3,2,1,0:T(8,128)S(1)}, u32[]{:S(2)}, u32[]{:S(2)}) collective-permute-start(f32[1,1,32,256]{3,2,1,0:T(8,128)S(1)} %get-tuple-element.658), channel_id=1, source_target_pairs={{0,1},{1,2},{2,3},{3,4},{4,5},{5,6},{6,7},{8,9},{9,10},{10,11},{11... | collective-permute-start | bytes 98312 | tf_op jit(solution)/shard_map/while/body/eval_jaxpr/ppermute | solution.py:19
  117.4 12.0 %collective-permute-start.6 = (f32[2,1,1,32,256]{4,3,2,1,0:T(8,128)S(1)}, f32[2,1,1,32,256]{4,3,2,1,0:T(8,128)S(1)}, u32[]{:S(2)}, u32[]{:S(2)}) collective-permute-start(f32[2,1,1,32,256]{4,3,2,1,0:T(8,128)S(1)} %get-tuple-element.661), channel_id=1, source_target_pairs={{1,0},{2,1},{3,2},{4,3},{5,4},{6,5},{7,6},{9,8},{10,9},{11,10},{12... | collective-permute-start | bytes 196616 | tf_op jit(solution)/shard_map/while/body/eval_jaxpr/ppermute | solution.py:21
  118.8 10.6 %collective-permute-start.7 = (f32[2,1,1,32,256]{4,3,2,1,0:T(8,128)S(1)}, f32[2,1,1,32,256]{4,3,2,1,0:T(8,128)S(1)}, u32[]{:S(2)}, u32[]{:S(2)}) collective-permute-start(f32[2,1,1,32,256]{4,3,2,1,0:T(8,128)S(1)} %get-tuple-element.662), channel_id=1, source_target_pairs={{0,1},{1,2},{2,3},{3,4},{4,5},{5,6},{6,7},{8,9},{9,10},{10,11},{11... | collective-permute-start | bytes 196616 | tf_op jit(solution)/shard_map/while/body/eval_jaxpr/ppermute | solution.py:19
  130.5 7.6 %collective-permute-start = (f32[2,1,1,32,256]{4,3,2,1,0:T(8,128)S(1)}, f32[2,1,1,32,256]{4,3,2,1,0:T(8,128)S(1)}, u32[]{:S(2)}, u32[]{:S(2)}) collective-permute-start(f32[2,1,1,32,256]{4,3,2,1,0:T(8,128)S(1)} %get-tuple-element.643), channel_id=1, source_target_pairs={{1,0},{2,1},{3,2},{4,3},{5,4},{6,5},{7,6},{9,8},{10,9},{11,10},{12... | collective-permute-start | bytes 196616 | tf_op jit(solution)/shard_map/while/body/eval_jaxpr/ppermute | solution.py:21
  131.8 8.0 %collective-permute-start.1 = (f32[2,1,1,32,256]{4,3,2,1,0:T(8,128)S(1)}, f32[2,1,1,32,256]{4,3,2,1,0:T(8,128)S(1)}, u32[]{:S(2)}, u32[]{:S(2)}) collective-permute-start(f32[2,1,1,32,256]{4,3,2,1,0:T(8,128)S(1)} %get-tuple-element.644), channel_id=1, source_target_pairs={{0,1},{1,2},{2,3},{3,4},{4,5},{5,6},{6,7},{8,9},{9,10},{10,11},{11... | collective-permute-start | bytes 196616 | tf_op jit(solution)/shard_map/while/body/eval_jaxpr/ppermute | solution.py:19
  149.7 7.3 %collective-permute-start.4 = (f32[1,1,32,256]{3,2,1,0:T(8,128)S(1)}, f32[1,1,32,256]{3,2,1,0:T(8,128)S(1)}, u32[]{:S(2)}, u32[]{:S(2)}) collective-permute-start(f32[1,1,32,256]{3,2,1,0:T(8,128)S(1)} %get-tuple-element.657), channel_id=1, source_target_pairs={{1,0},{2,1},{3,2},{4,3},{5,4},{6,5},{7,6},{9,8},{10,9},{11,10},{12... | collective-permute-start | bytes 98312 | tf_op jit(solution)/shard_map/while/body/eval_jaxpr/ppermute | solution.py:21
  151.0 7.6 %collective-permute-start.5 = (f32[1,1,32,256]{3,2,1,0:T(8,128)S(1)}, f32[1,1,32,256]{3,2,1,0:T(8,128)S(1)}, u32[]{:S(2)}, u32[]{:S(2)}) collective-permute-start(f32[1,1,32,256]{3,2,1,0:T(8,128)S(1)} %get-tuple-element.658), channel_id=1, source_target_pairs={{0,1},{1,2},{2,3},{3,4},{4,5},{5,6},{6,7},{8,9},{9,10},{10,11},{11... | collective-permute-start | bytes 98312 | tf_op jit(solution)/shard_map/while/body/eval_jaxpr/ppermute | solution.py:19
  160.8 12.0 %collective-permute-start.6 = (f32[2,1,1,32,256]{4,3,2,1,0:T(8,128)S(1)}, f32[2,1,1,32,256]{4,3,2,1,0:T(8,128)S(1)}, u32[]{:S(2)}, u32[]{:S(2)}) collective-permute-start(f32[2,1,1,32,256]{4,3,2,1,0:T(8,128)S(1)} %get-tuple-element.661), channel_id=1, source_target_pairs={{1,0},{2,1},{3,2},{4,3},{5,4},{6,5},{7,6},{9,8},{10,9},{11,10},{12... | collective-permute-start | bytes 196616 | tf_op jit(solution)/shard_map/while/body/eval_jaxpr/ppermute | solution.py:21
  162.2 10.5 %collective-permute-start.7 = (f32[2,1,1,32,256]{4,3,2,1,0:T(8,128)S(1)}, f32[2,1,1,32,256]{4,3,2,1,0:T(8,128)S(1)}, u32[]{:S(2)}, u32[]{:S(2)}) collective-permute-start(f32[2,1,1,32,256]{4,3,2,1,0:T(8,128)S(1)} %get-tuple-element.662), channel_id=1, source_target_pairs={{0,1},{1,2},{2,3},{3,4},{4,5},{5,6},{6,7},{8,9},{9,10},{10,11},{11... | collective-permute-start | bytes 196616 | tf_op jit(solution)/shard_map/while/body/eval_jaxpr/ppermute | solution.py:19
  173.9 7.4 %collective-permute-start = (f32[2,1,1,32,256]{4,3,2,1,0:T(8,128)S(1)}, f32[2,1,1,32,256]{4,3,2,1,0:T(8,128)S(1)}, u32[]{:S(2)}, u32[]{:S(2)}) collective-permute-start(f32[2,1,1,32,256]{4,3,2,1,0:T(8,128)S(1)} %get-tuple-element.643), channel_id=1, source_target_pairs={{1,0},{2,1},{3,2},{4,3},{5,4},{6,5},{7,6},{9,8},{10,9},{11,10},{12... | collective-permute-start | bytes 196616 | tf_op jit(solution)/shard_map/while/body/eval_jaxpr/ppermute | solution.py:21
  175.2 7.6 %collective-permute-start.1 = (f32[2,1,1,32,256]{4,3,2,1,0:T(8,128)S(1)}, f32[2,1,1,32,256]{4,3,2,1,0:T(8,128)S(1)}, u32[]{:S(2)}, u32[]{:S(2)}) collective-permute-start(f32[2,1,1,32,256]{4,3,2,1,0:T(8,128)S(1)} %get-tuple-element.644), channel_id=1, source_target_pairs={{0,1},{1,2},{2,3},{3,4},{4,5},{5,6},{6,7},{8,9},{9,10},{10,11},{11... | collective-permute-start | bytes 196616 | tf_op jit(solution)/shard_map/while/body/eval_jaxpr/ppermute | solution.py:19
  192.8 7.1 %collective-permute-start.4 = (f32[1,1,32,256]{3,2,1,0:T(8,128)S(1)}, f32[1,1,32,256]{3,2,1,0:T(8,128)S(1)}, u32[]{:S(2)}, u32[]{:S(2)}) collective-permute-start(f32[1,1,32,256]{3,2,1,0:T(8,128)S(1)} %get-tuple-element.657), channel_id=1, source_target_pairs={{1,0},{2,1},{3,2},{4,3},{5,4},{6,5},{7,6},{9,8},{10,9},{11,10},{12... | collective-permute-start | bytes 98312 | tf_op jit(solution)/shard_map/while/body/eval_jaxpr/ppermute | solution.py:21
  194.1 7.4 %collective-permute-start.5 = (f32[1,1,32,256]{3,2,1,0:T(8,128)S(1)}, f32[1,1,32,256]{3,2,1,0:T(8,128)S(1)}, u32[]{:S(2)}, u32[]{:S(2)}) collective-permute-start(f32[1,1,32,256]{3,2,1,0:T(8,128)S(1)} %get-tuple-element.658), channel_id=1, source_target_pairs={{0,1},{1,2},{2,3},{3,4},{4,5},{5,6},{6,7},{8,9},{9,10},{10,11},{11... | collective-permute-start | bytes 98312 | tf_op jit(solution)/shard_map/while/body/eval_jaxpr/ppermute | solution.py:19
  203.7 12.0 %collective-permute-start.6 = (f32[2,1,1,32,256]{4,3,2,1,0:T(8,128)S(1)}, f32[2,1,1,32,256]{4,3,2,1,0:T(8,128)S(1)}, u32[]{:S(2)}, u32[]{:S(2)}) collective-permute-start(f32[2,1,1,32,256]{4,3,2,1,0:T(8,128)S(1)} %get-tuple-element.661), channel_id=1, source_target_pairs={{1,0},{2,1},{3,2},{4,3},{5,4},{6,5},{7,6},{9,8},{10,9},{11,10},{12... | collective-permute-start | bytes 196616 | tf_op jit(solution)/shard_map/while/body/eval_jaxpr/ppermute | solution.py:21
  205.1 10.6 %collective-permute-start.7 = (f32[2,1,1,32,256]{4,3,2,1,0:T(8,128)S(1)}, f32[2,1,1,32,256]{4,3,2,1,0:T(8,128)S(1)}, u32[]{:S(2)}, u32[]{:S(2)}) collective-permute-start(f32[2,1,1,32,256]{4,3,2,1,0:T(8,128)S(1)} %get-tuple-element.662), channel_id=1, source_target_pairs={{0,1},{1,2},{2,3},{3,4},{4,5},{5,6},{6,7},{8,9},{9,10},{10,11},{11... | collective-permute-start | bytes 196616 | tf_op jit(solution)/shard_map/while/body/eval_jaxpr/ppermute | solution.py:19
  229.0 75.5 %all-to-all-start.2 = ((f32[4,1,4,32,256]{4,3,2,1,0:T(8,128)}), f32[4,1,4,32,256]{4,3,2,1,0:T(8,128)S(1)}, u32[]{:S(2)}, u32[]{:S(2)}) async-start(f32[4,1,4,32,256]{4,3,2,1,0:T(8,128)} %get-tuple-element.381), calls=%async_computation.2 | async-start | bytes 1048576 | tf_op jit(solution)/shard_map/all_to_all | solution.py:190
  (32 other events, 182.1 us)
